TPU v7x, 32 devices: a whole 2x2x4 slice. The times are simulated.
32 devices in a mesh: cond: 2 (over x), gx: 4 (over y, core), yz: 4 (over z).
Axes of the slice: x: 2, y: 2, z: 4, core: 2. Of those that a mesh axis runs over, the one named last changes fastest.
Arguments:
- adjoint: float32 [2, 5, 32, 64, 256], P('cond', None, 'gx', 'yz'), may hold values from -6 to 6
- objective_gradient: float32 [2, 5, 32, 64, 256], P('cond', None, 'gx', 'yz'), may hold values from -6 to 6
- diagonal: float32 [32, 64, 256], P('gx', 'yz'), may hold values from 4 to 12
- flux_blocks: float32 [2, 6, 5, 5], P('cond'), may hold values from -1 to 1
- flux_sensitivity: bfloat16 [2, 5, 32, 64, 256], P('cond', None, 'gx', 'yz'), may hold values from -6 to 6
- surface_mask: int32 [32, 64, 256], P('gx', 'yz'), may hold values 0 or 1
- patch_band_slot: int32 [32, 64], P('gx', 'yz'), may hold values from 0 to 62
- design_basis: float32 [256, 128], replicated, may hold values from -0.046875 to 0.046875
- condition_weights: int32 [2], replicated, may hold values from 1 to 999, as said below
Outputs:
- smoothed: float32 [2, 5, 32, 64, 256], P('cond', None, 'gx', 'yz')
- residual: float32 [2, 5, 32, 64, 256], P('cond', None, 'gx', 'yz')
- design_gradient: float32 [4096], P(('gx', 'yz'))
Inputs may be any that keep to these rules, and one draw needn't show every extreme that they name: `condition_weights`: positive integer weights; one condition has weight 999.
All inputs are finite; a program needn't handle non-finite values. No bound on the sum of `surface_mask` on one device may be relied on, other than what follows from the above.
Results may differ from a plain program's by a relative error of at most 0.0003.
Values sent between devices are 32-bit elements; how exact they have to be, the bound alone decides.
A program may use at most 64 MiB of HBM per device.

v0:
```python
import jax
import jax.numpy as jnp
from jax import lax
from jax.sharding import PartitionSpec as P

NDES = 4096


relaxation = 0.8
neighbour_starts = ((2, 1, 1), (0, 1, 1), (1, 2, 1), (1, 0, 1), (1, 1, 2), (1, 1, 0))


def with_halo(block, sides, width):
    for axis, dim in sides:
        count = lax.axis_size(axis)
        forward = [(i, i + 1) for i in range(count - 1)]
        backward = [(target, source) for source, target in forward]
        low = lax.ppermute(
            lax.slice_in_dim(block, block.shape[dim] - width, None, axis=dim), axis, forward
        )
        high = lax.ppermute(lax.slice_in_dim(block, 0, width, axis=dim), axis, backward)
        block = jnp.concatenate([low, block, high], axis=dim)
    return block


def apply_operator(padded_field, diagonal, blocks):
    size_x = padded_field.shape[1] - 2
    size_y = padded_field.shape[2] - 2
    size_z = padded_field.shape[3] - 2
    result = diagonal * padded_field[:, 1:-1, 1:-1, 1:-1]
    for direction in range(6):
        start_x, start_y, start_z = neighbour_starts[direction]
        shifted = padded_field[
            :, start_x : start_x + size_x, start_y : start_y + size_y, start_z : start_z + size_z
        ]
        result = result - jnp.einsum(
            "ec,exyz->cxyz", blocks[direction], shifted, precision=lax.Precision.HIGHEST
        )
    return result


def spread_bands(slot_lookup):
    halfway = slot_lookup.shape[1] // 2
    first_half = jnp.pad(slot_lookup[:, :halfway], ((0, 1), (0, 0)))
    second_half = jnp.pad(slot_lookup[:, halfway:], ((1, 0), (0, 0)))
    return (first_half + second_half).reshape(-1)


def pad_third(values):
    return jnp.pad(values, ((0, 0), (0, 0), (0, 0), (1, 1)))


def local(
    adjoint,
    objective_gradient,
    diagonal,
    flux_blocks,
    flux_sensitivity,
    surface_mask,
    patch_band_slot,
    design_basis,
    condition_weights,
):
    blocks = flux_blocks[0]
    source = objective_gradient[0]
    start_field = adjoint[0]

    def operate(values):
        haloed = with_halo(values, (("gx", 1), ("yz", 2)), 1)
        return apply_operator(pad_third(haloed), diagonal, blocks)

    relaxed = start_field + relaxation * (source - operate(start_field)) / diagonal
    smoothed = relaxed + relaxation * (source - operate(relaxed)) / diagonal
    residual = source - operate(smoothed)
    surface = surface_mask.astype(jnp.float32) * jnp.sum(
        smoothed * flux_sensitivity[0].astype(jnp.float32), axis=0
    )
    projected_gradient = jnp.dot(
        surface.reshape(-1, surface.shape[-1]),
        design_basis,
        precision=lax.Precision.HIGHEST,
        preferred_element_type=jnp.float32,
    )
    slot_count = 2 * NDES // design_basis.shape[1] - 1
    onehot = (jnp.arange(slot_count)[:, None] == patch_band_slot.reshape(1, -1)).astype(jnp.float32)
    slot_lookup = jnp.dot(
        onehot,
        projected_gradient,
        precision=lax.Precision.HIGHEST,
        preferred_element_type=jnp.float32,
    )
    gradient = spread_bands(slot_lookup)
    weights_float = condition_weights.astype(jnp.float32)
    picked = jnp.arange(weights_float.shape[0]) == lax.axis_index("cond")
    local_portion = jnp.sum(jnp.where(picked, weights_float, 0.0)) / jnp.sum(weights_float)
    summed = lax.psum(local_portion * gradient, ("cond", "gx", "yz"))
    pieces = NDES // lax.axis_size(("gx", "yz"))
    design_gradient = lax.dynamic_slice_in_dim(
        summed, lax.axis_index(("gx", "yz")) * pieces, pieces, 0
    )
    return (smoothed[None], residual[None], design_gradient)


def solution(mesh):
    placed = (
        P("cond", None, "gx", "yz", None),
        P("cond", None, "gx", "yz", None),
        P("gx", "yz", None),
        P("cond", None, None, None),
        P("cond", None, "gx", "yz", None),
        P("gx", "yz", None),
        P("gx", "yz"),
        P(),
        P(),
    )
    return jax.shard_map(
        local,
        mesh=mesh,
        in_specs=placed,
        out_specs=(
            P("cond", None, "gx", "yz", None),
            P("cond", None, "gx", "yz", None),
            P(("gx", "yz")),
        ),
        check_vma=False,
    )
```

profile of v0, /device:TPU:0, one launch (start us, length us, event | category | flops | bytes accessed | tf_op | source)
XLA Modules:
  0.0 115.3 jit_solution(11190379338171602337)
XLA Ops:
  0.7 1.5 %copy.88 = f32[1,5,8,16,256]{4,1,3,2,0:T(8,128)S(1)} copy(f32[1,5,8,16,256]{4,3,2,1,0:T(8,128)} %param.9) | data formatting | bytes 1310720 | tf_op args[0]
  2.2 1.3 %collective-permute-start = (f32[5,1,16,256]{3,0,2,1:T(8,128)S(1)}, f32[5,1,16,256]{3,0,2,1:T(8,128)S(1)}, u32[]{:S(2)}, u32[]{:S(2)}) collective-permute-start(f32[5,1,16,256]{3,0,2,1:T(8,128)S(1)} %get-tuple-element.19), channel_id=1, source_target_pairs={{4,0},{8,4},{12,8},{5,1},{9,5},{13,9},{6,2},{10,6},{14,10},{7,3},{... | collective-permute-start | bytes 245768 | tf_op jit(solution)/shard_map/ppermute | solution.py:21
  3.5 3.0 %collective-permute-start.1 = (f32[5,1,16,256]{3,0,2,1:T(8,128)S(1)}, f32[5,1,16,256]{3,0,2,1:T(8,128)S(1)}, u32[]{:S(2)}, u32[]{:S(2)}) collective-permute-start(f32[5,1,16,256]{3,0,2,1:T(8,128)S(1)} %get-tuple-element.18), channel_id=1, source_target_pairs={{0,4},{4,8},{8,12},{1,5},{5,9},{9,13},{2,6},{6,10},{10,14},{3,7},{... | collective-permute-start | bytes 245768 | tf_op jit(solution)/shard_map/ppermute | solution.py:18
  6.6 0.2 fusion.157
  6.8 0.1 copy.82
  6.9 0.1 copy.81
  7.0 0.1 copy.80
  7.7 1.3 %collective-permute-start.2 = (f32[5,10,1,256]{3,0,2,1:T(8,128)S(1)}, f32[5,10,1,256]{3,0,2,1:T(8,128)S(1)}, u32[]{:S(2)}, u32[]{:S(2)}) collective-permute-start(f32[5,10,1,256]{3,0,2,1:T(8,128)S(1)} %get-tuple-element.13), channel_id=1, source_target_pairs={{1,0},{2,1},{3,2},{5,4},{6,5},{7,6},{9,8},{10,9},{11,10},{13,12},{... | collective-permute-start | bytes 153608 | tf_op jit(solution)/shard_map/ppermute | solution.py:21
  9.0 5.6 %collective-permute-start.3 = (f32[5,10,1,256]{3,0,2,1:T(8,128)S(1)}, f32[5,10,1,256]{3,0,2,1:T(8,128)S(1)}, u32[]{:S(2)}, u32[]{:S(2)}) collective-permute-start(f32[5,10,1,256]{3,0,2,1:T(8,128)S(1)} %get-tuple-element.12), channel_id=1, source_target_pairs={{0,1},{1,2},{2,3},{4,5},{5,6},{6,7},{8,9},{9,10},{10,11},{12,13},{... | collective-permute-start | bytes 153608 | tf_op jit(solution)/shard_map/ppermute | solution.py:18
  14.6 1.1 convolution_bitcast_fusion.4
  15.7 0.9 collective-permute-done.3
  16.6 0.6 select_maximum_fusion.8
  17.3 1.0 convolution_bitcast_fusion.10
  18.3 1.2 %convolution_bitcast_fusion.11 = f32[5,8,16,256]{3,0,2,1:T(8,128)S(1)} fusion(f32[5,10,18,258]{3,0,2,1:T(8,128)S(1)} %select_maximum_fusion.8, f32[1,1,5,5]{3,2,1,0:T(8,128)S(1)} %copy.81), kind=kOutput, calls=%fused_computation.86 | convolution fusion | flops 9830400 | bytes 1708032 | tf_op jit(solution)/shard_map/ec,exyz->cxyz/dot_general | solution.py:36
  19.6 1.1 fusion.61
  20.7 1.1 fusion.64
  21.8 2.0 %fusion.94 = f32[5,8,16,256]{3,0,2,1:T(8,128)S(1)} fusion(f32[5,8,16,256]{3,0,2,1:T(8,128)S(1)} %bitcast.184, f32[5,8,16,256]{3,0,2,1:T(8,128)S(1)} %convolution_bitcast_fusion.10, f32[5,8,16,256]{3,0,2,1:T(8,128)S(1)} %convolution_bitcast_fusion.11, f32[5,8,16,256]{3,0,2,1:T(8,128)S(1)} %fusion.61, f32[5,8,16,256]{3,0,2,1:T(8,128)S(1)} %fusion.64, ...), kind=kOutput, calls=%fused_computation.108 | convolution fusion | flops 11816960 | bytes 5455972 | tf_op jit(solution)/shard_map/ec,exyz->cxyz/dot_general | solution.py:36
  23.8 1.3 %collective-permute-start.4 = (f32[5,1,16,256]{3,0,2,1:T(8,128)S(1)}, f32[5,1,16,256]{3,0,2,1:T(8,128)S(1)}, u32[]{:S(2)}, u32[]{:S(2)}) collective-permute-start(f32[5,1,16,256]{3,0,2,1:T(8,128)S(1)} %get-tuple-element.17), channel_id=1, source_target_pairs={{4,0},{8,4},{12,8},{5,1},{9,5},{13,9},{6,2},{10,6},{14,10},{7,3},{... | collective-permute-start | bytes 245768 | tf_op jit(solution)/shard_map/ppermute | solution.py:21
  25.1 3.8 %collective-permute-start.5 = (f32[5,1,16,256]{3,0,2,1:T(8,128)S(1)}, f32[5,1,16,256]{3,0,2,1:T(8,128)S(1)}, u32[]{:S(2)}, u32[]{:S(2)}) collective-permute-start(f32[5,1,16,256]{3,0,2,1:T(8,128)S(1)} %get-tuple-element.16), channel_id=1, source_target_pairs={{0,4},{4,8},{8,12},{1,5},{5,9},{9,13},{2,6},{6,10},{10,14},{3,7},{... | collective-permute-start | bytes 245768 | tf_op jit(solution)/shard_map/ppermute | solution.py:18
  28.9 0.6 convert_reduce_fusion
  30.9 1.3 %collective-permute-start.6 = (f32[5,10,1,256]{3,0,2,1:T(8,128)S(1)}, f32[5,10,1,256]{3,0,2,1:T(8,128)S(1)}, u32[]{:S(2)}, u32[]{:S(2)}) collective-permute-start(f32[5,10,1,256]{3,0,2,1:T(8,128)S(1)} %get-tuple-element.11), channel_id=1, source_target_pairs={{1,0},{2,1},{3,2},{5,4},{6,5},{7,6},{9,8},{10,9},{11,10},{13,12},{... | collective-permute-start | bytes 153608 | tf_op jit(solution)/shard_map/ppermute | solution.py:21
  32.2 4.8 %collective-permute-start.7 = (f32[5,10,1,256]{3,0,2,1:T(8,128)S(1)}, f32[5,10,1,256]{3,0,2,1:T(8,128)S(1)}, u32[]{:S(2)}, u32[]{:S(2)}) collective-permute-start(f32[5,10,1,256]{3,0,2,1:T(8,128)S(1)} %get-tuple-element.10), channel_id=1, source_target_pairs={{0,1},{1,2},{2,3},{4,5},{5,6},{6,7},{8,9},{9,10},{10,11},{12,13},{... | collective-permute-start | bytes 153608 | tf_op jit(solution)/shard_map/ppermute | solution.py:18
  37.0 1.1 convolution_bitcast_fusion.2
  38.1 0.8 collective-permute-done.7
  38.9 0.6 select_maximum_fusion.4
  39.5 1.0 convolution_bitcast_fusion.8
  40.6 1.2 %convolution_bitcast_fusion.9 = f32[5,8,16,256]{3,0,2,1:T(8,128)S(1)} fusion(f32[5,10,18,258]{3,0,2,1:T(8,128)S(1)} %select_maximum_fusion.4, f32[1,1,5,5]{3,2,1,0:T(8,128)S(1)} %copy.81), kind=kOutput, calls=%fused_computation.84 | convolution fusion | flops 9830400 | bytes 1708032 | tf_op jit(solution)/shard_map/ec,exyz->cxyz/dot_general | solution.py:36
  41.8 1.1 fusion.55
  42.9 1.1 fusion.58
  44.0 2.2 %fusion.119 = (f32[8,16,256]{2,1,0:T(8,128)S(1)}, f32[5,8,16,256]{3,0,2,1:T(8,128)S(1)}) fusion(bf16[1,5,8,16,256]{4,3,2,1,0:T(8,128)(2,1)S(1)} %copy-done.3, f32[5,8,16,256]{3,0,2,1:T(8,128)S(1)} %fusion.94, f32[5,8,16,256]{3,0,2,1:T(8,128)S(1)} %convolution_bitcast_fusion.8, f32[5,8,16,256]{3,0,2,1:T(8,128)S(1)} %convolution_bitcast_fusion.9, ...), kind=kOutput, calls=%fused_computation.134 | convolution fusion | flops 12275712 | bytes 5914724 | tf_op jit(solution)/shard_map/ec,exyz->cxyz/dot_general | solution.py:36
  46.2 1.0 copy.39
  47.2 1.3 %collective-permute-start.8 = (f32[5,1,16,256]{3,0,2,1:T(8,128)S(1)}, f32[5,1,16,256]{3,0,2,1:T(8,128)S(1)}, u32[]{:S(2)}, u32[]{:S(2)}) collective-permute-start(f32[5,1,16,256]{3,0,2,1:T(8,128)S(1)} %get-tuple-element.15), channel_id=1, source_target_pairs={{4,0},{8,4},{12,8},{5,1},{9,5},{13,9},{6,2},{10,6},{14,10},{7,3},{... | collective-permute-start | bytes 245768 | tf_op jit(solution)/shard_map/ppermute | solution.py:21
  48.5 5.6 %collective-permute-start.9 = (f32[5,1,16,256]{3,0,2,1:T(8,128)S(1)}, f32[5,1,16,256]{3,0,2,1:T(8,128)S(1)}, u32[]{:S(2)}, u32[]{:S(2)}) collective-permute-start(f32[5,1,16,256]{3,0,2,1:T(8,128)S(1)} %get-tuple-element.14), channel_id=1, source_target_pairs={{0,4},{4,8},{8,12},{1,5},{5,9},{9,13},{2,6},{6,10},{10,14},{3,7},{... | collective-permute-start | bytes 245768 | tf_op jit(solution)/shard_map/ppermute | solution.py:18
  54.1 0.3 fusion.158
  54.4 0.2 fusion.120
  54.8 43.9 %psum.7 = f32[4096]{0:T(1024)S(1)} all-reduce(f32[4096]{0:T(1024)S(1)} %mul.57), channel_id=1, replica_groups=mesh['cond'=2,'gx'=4,'yz'=4] {'cond','gx','yz'}, use_global_device_ids=true, to_apply=%region_3.4 | all-reduce | flops 4096 | bytes 32768 | tf_op jit(solution)/shard_map/psum | solution.py:96
  98.6 0.6 dynamic_slice.3
  99.3 1.3 %collective-permute-start.10 = (f32[5,10,1,256]{3,0,2,1:T(8,128)S(1)}, f32[5,10,1,256]{3,0,2,1:T(8,128)S(1)}, u32[]{:S(2)}, u32[]{:S(2)}) collective-permute-start(f32[5,10,1,256]{3,0,2,1:T(8,128)S(1)} %get-tuple-element.9), channel_id=1, source_target_pairs={{1,0},{2,1},{3,2},{5,4},{6,5},{7,6},{9,8},{10,9},{11,10},{13,12},{... | collective-permute-start | bytes 153608 | tf_op jit(solution)/shard_map/ppermute | solution.py:21
  100.6 4.8 %collective-permute-start.11 = (f32[5,10,1,256]{3,0,2,1:T(8,128)S(1)}, f32[5,10,1,256]{3,0,2,1:T(8,128)S(1)}, u32[]{:S(2)}, u32[]{:S(2)}) collective-permute-start(f32[5,10,1,256]{3,0,2,1:T(8,128)S(1)} %get-tuple-element.8), channel_id=1, source_target_pairs={{0,1},{1,2},{2,3},{4,5},{5,6},{6,7},{8,9},{9,10},{10,11},{12,13},{... | collective-permute-start | bytes 153608 | tf_op jit(solution)/shard_map/ppermute | solution.py:18
  105.4 1.1 convolution_bitcast_fusion
  106.5 0.7 collective-permute-done.11
  107.2 0.6 select_maximum_fusion
  107.9 1.0 convolution_bitcast_fusion.6
  108.9 1.2 %convolution_bitcast_fusion.7 = f32[5,8,16,256]{3,0,2,1:T(8,128)S(1)} fusion(f32[5,10,18,258]{3,0,2,1:T(8,128)S(1)} %select_maximum_fusion, f32[1,1,5,5]{3,2,1,0:T(8,128)S(1)} %copy.81), kind=kOutput, calls=%fused_computation.82 | convolution fusion | flops 9830400 | bytes 1708032 | tf_op jit(solution)/shard_map/ec,exyz->cxyz/dot_general | solution.py:36
  110.1 1.1 fusion.49
  111.2 1.1 fusion.52
  112.3 2.0 %fusion.86 = f32[1,5,8,16,256]{4,1,3,2,0:T(8,128)S(1)} fusion(f32[5,8,16,256]{3,0,2,1:T(8,128)S(1)} %convolution_bitcast_fusion.6, f32[5,8,16,256]{3,0,2,1:T(8,128)S(1)} %convolution_bitcast_fusion.7, f32[5,8,16,256]{3,0,2,1:T(8,128)S(1)} %fusion.49, f32[5,8,16,256]{3,0,2,1:T(8,128)S(1)} %fusion.52, f32[5,8,16,256]{3,0,2,1:T(8,128)S(1)} %convolution_bitcast_fusion, ...), kind=kOutput, calls=%fused_computation.100 | convolution fusion | flops 11325440 | bytes 5455972 | tf_op jit(solution)/shard_map/ec,exyz->cxyz/dot_general | solution.py:36
  114.3 1.0 copy.40
  (39 shorter events, 0.9 us)
Async XLA Ops:
  0.6 53.5 %copy-start = (f32[256,128]{1,0:T(8,128)S(1)}, f32[256,128]{1,0:T(8,128)}, u32[]{:S(2)}) copy-start(f32[256,128]{1,0:T(8,128)} %param.16) | copy-start | bytes 393220
  0.6 5.9 %copy-start.4 = (f32[1,6,5,5]{1,0,3,2:T(1,128)S(1)}, f32[1,6,5,5]{1,0,3,2:T(1,128)}, u32[]{:S(2)}) copy-start(f32[1,6,5,5]{1,0,3,2:T(1,128)} %param.12) | copy-start | bytes 1804
  0.7 6.9 %copy-start.6 = (s32[8,16]{1,0:T(8,128)S(1)}, s32[8,16]{1,0:T(8,128)}, u32[]{:S(2)}) copy-start(s32[8,16]{1,0:T(8,128)} %param.15) | copy-start | bytes 1540
  2.2 5.4 %collective-permute-start = (f32[5,1,16,256]{3,0,2,1:T(8,128)S(1)}, f32[5,1,16,256]{3,0,2,1:T(8,128)S(1)}, u32[]{:S(2)}, u32[]{:S(2)}) collective-permute-start(f32[5,1,16,256]{3,0,2,1:T(8,128)S(1)} %get-tuple-element.19), channel_id=1, source_target_pairs={{4,0},{8,4},{12,8},{5,1},{9,5},{13,9},{6,2},{10,6},{14,10},{7,3},{... | collective-permute-start | bytes 245768 | tf_op jit(solution)/shard_map/ppermute | solution.py:21
  3.5 4.2 %collective-permute-start.1 = (f32[5,1,16,256]{3,0,2,1:T(8,128)S(1)}, f32[5,1,16,256]{3,0,2,1:T(8,128)S(1)}, u32[]{:S(2)}, u32[]{:S(2)}) collective-permute-start(f32[5,1,16,256]{3,0,2,1:T(8,128)S(1)} %get-tuple-element.18), channel_id=1, source_target_pairs={{0,4},{4,8},{8,12},{1,5},{5,9},{9,13},{2,6},{6,10},{10,14},{3,7},{... | collective-permute-start | bytes 245768 | tf_op jit(solution)/shard_map/ppermute | solution.py:18
  7.7 8.0 %collective-permute-start.2 = (f32[5,10,1,256]{3,0,2,1:T(8,128)S(1)}, f32[5,10,1,256]{3,0,2,1:T(8,128)S(1)}, u32[]{:S(2)}, u32[]{:S(2)}) collective-permute-start(f32[5,10,1,256]{3,0,2,1:T(8,128)S(1)} %get-tuple-element.13), channel_id=1, source_target_pairs={{1,0},{2,1},{3,2},{5,4},{6,5},{7,6},{9,8},{10,9},{11,10},{13,12},{... | collective-permute-start | bytes 153608 | tf_op jit(solution)/shard_map/ppermute | solution.py:21
  9.0 7.6 %collective-permute-start.3 = (f32[5,10,1,256]{3,0,2,1:T(8,128)S(1)}, f32[5,10,1,256]{3,0,2,1:T(8,128)S(1)}, u32[]{:S(2)}, u32[]{:S(2)}) collective-permute-start(f32[5,10,1,256]{3,0,2,1:T(8,128)S(1)} %get-tuple-element.12), channel_id=1, source_target_pairs={{0,1},{1,2},{2,3},{4,5},{5,6},{6,7},{8,9},{9,10},{10,11},{12,13},{... | collective-permute-start | bytes 153608 | tf_op jit(solution)/shard_map/ppermute | solution.py:18
  19.6 2.2 %copy-start.1 = (f32[1,5,8,16,256]{4,3,2,1,0:T(8,128)S(1)}, f32[1,5,8,16,256]{4,3,2,1,0:T(8,128)}, u32[]{:S(2)}) copy-start(f32[1,5,8,16,256]{4,3,2,1,0:T(8,128)} %param.10) | copy-start | bytes 1966084
  19.6 2.2 %copy-start.2 = (f32[8,16,256]{2,1,0:T(8,128)S(1)}, f32[8,16,256]{2,1,0:T(8,128)}, u32[]{:S(2)}) copy-start(f32[8,16,256]{2,1,0:T(8,128)} %param.11) | copy-start | bytes 393220
  21.8 7.2 %copy-start.7 = (s32[2]{0:T(128)S(1)}, s32[2]{0:T(128)}, u32[]{:S(2)}) copy-start(s32[2]{0:T(128)} %param.17) | copy-start | bytes 28
  23.8 7.1 %collective-permute-start.4 = (f32[5,1,16,256]{3,0,2,1:T(8,128)S(1)}, f32[5,1,16,256]{3,0,2,1:T(8,128)S(1)}, u32[]{:S(2)}, u32[]{:S(2)}) collective-permute-start(f32[5,1,16,256]{3,0,2,1:T(8,128)S(1)} %get-tuple-element.17), channel_id=1, source_target_pairs={{4,0},{8,4},{12,8},{5,1},{9,5},{13,9},{6,2},{10,6},{14,10},{7,3},{... | collective-permute-start | bytes 245768 | tf_op jit(solution)/shard_map/ppermute | solution.py:21
  25.1 5.8 %collective-permute-start.5 = (f32[5,1,16,256]{3,0,2,1:T(8,128)S(1)}, f32[5,1,16,256]{3,0,2,1:T(8,128)S(1)}, u32[]{:S(2)}, u32[]{:S(2)}) collective-permute-start(f32[5,1,16,256]{3,0,2,1:T(8,128)S(1)} %get-tuple-element.16), channel_id=1, source_target_pairs={{0,4},{4,8},{8,12},{1,5},{5,9},{9,13},{2,6},{6,10},{10,14},{3,7},{... | collective-permute-start | bytes 245768 | tf_op jit(solution)/shard_map/ppermute | solution.py:18
  30.9 7.2 %collective-permute-start.6 = (f32[5,10,1,256]{3,0,2,1:T(8,128)S(1)}, f32[5,10,1,256]{3,0,2,1:T(8,128)S(1)}, u32[]{:S(2)}, u32[]{:S(2)}) collective-permute-start(f32[5,10,1,256]{3,0,2,1:T(8,128)S(1)} %get-tuple-element.11), channel_id=1, source_target_pairs={{1,0},{2,1},{3,2},{5,4},{6,5},{7,6},{9,8},{10,9},{11,10},{13,12},{... | collective-permute-start | bytes 153608 | tf_op jit(solution)/shard_map/ppermute | solution.py:21
  32.2 6.7 %collective-permute-start.7 = (f32[5,10,1,256]{3,0,2,1:T(8,128)S(1)}, f32[5,10,1,256]{3,0,2,1:T(8,128)S(1)}, u32[]{:S(2)}, u32[]{:S(2)}) collective-permute-start(f32[5,10,1,256]{3,0,2,1:T(8,128)S(1)} %get-tuple-element.10), channel_id=1, source_target_pairs={{0,1},{1,2},{2,3},{4,5},{5,6},{6,7},{8,9},{9,10},{10,11},{12,13},{... | collective-permute-start | bytes 153608 | tf_op jit(solution)/shard_map/ppermute | solution.py:18
  41.8 2.2 %copy-start.3 = (bf16[1,5,8,16,256]{4,3,2,1,0:T(8,128)(2,1)S(1)}, bf16[1,5,8,16,256]{4,3,2,1,0:T(8,128)(2,1)}, u32[]{:S(2)}) copy-start(bf16[1,5,8,16,256]{4,3,2,1,0:T(8,128)(2,1)} %param.13) | copy-start | bytes 983044
  46.1 7.9 %copy-start.5 = (s32[8,16,256]{2,1,0:T(8,128)S(1)}, s32[8,16,256]{2,1,0:T(8,128)}, u32[]{:S(2)}) copy-start(s32[8,16,256]{2,1,0:T(8,128)} %param.14) | copy-start | bytes 393220
  47.2 52.1 %collective-permute-start.8 = (f32[5,1,16,256]{3,0,2,1:T(8,128)S(1)}, f32[5,1,16,256]{3,0,2,1:T(8,128)S(1)}, u32[]{:S(2)}, u32[]{:S(2)}) collective-permute-start(f32[5,1,16,256]{3,0,2,1:T(8,128)S(1)} %get-tuple-element.15), channel_id=1, source_target_pairs={{4,0},{8,4},{12,8},{5,1},{9,5},{13,9},{6,2},{10,6},{14,10},{7,3},{... | collective-permute-start | bytes 245768 | tf_op jit(solution)/shard_map/ppermute | solution.py:21
  48.5 50.8 %collective-permute-start.9 = (f32[5,1,16,256]{3,0,2,1:T(8,128)S(1)}, f32[5,1,16,256]{3,0,2,1:T(8,128)S(1)}, u32[]{:S(2)}, u32[]{:S(2)}) collective-permute-start(f32[5,1,16,256]{3,0,2,1:T(8,128)S(1)} %get-tuple-element.14), channel_id=1, source_target_pairs={{0,4},{4,8},{8,12},{1,5},{5,9},{9,13},{2,6},{6,10},{10,14},{3,7},{... | collective-permute-start | bytes 245768 | tf_op jit(solution)/shard_map/ppermute | solution.py:18
  99.3 7.2 %collective-permute-start.10 = (f32[5,10,1,256]{3,0,2,1:T(8,128)S(1)}, f32[5,10,1,256]{3,0,2,1:T(8,128)S(1)}, u32[]{:S(2)}, u32[]{:S(2)}) collective-permute-start(f32[5,10,1,256]{3,0,2,1:T(8,128)S(1)} %get-tuple-element.9), channel_id=1, source_target_pairs={{1,0},{2,1},{3,2},{5,4},{6,5},{7,6},{9,8},{10,9},{11,10},{13,12},{... | collective-permute-start | bytes 153608 | tf_op jit(solution)/shard_map/ppermute | solution.py:21
  100.6 6.6 %collective-permute-start.11 = (f32[5,10,1,256]{3,0,2,1:T(8,128)S(1)}, f32[5,10,1,256]{3,0,2,1:T(8,128)S(1)}, u32[]{:S(2)}, u32[]{:S(2)}) collective-permute-start(f32[5,10,1,256]{3,0,2,1:T(8,128)S(1)} %get-tuple-element.8), channel_id=1, source_target_pairs={{0,1},{1,2},{2,3},{4,5},{5,6},{6,7},{8,9},{9,10},{10,11},{12,13},{... | collective-permute-start | bytes 153608 | tf_op jit(solution)/shard_map/ppermute | solution.py:18
where the time goes:
time: 116 us; the launch traced here: 115 us
  blocking collectives  43.9 us (38%)
  starting transfers between devices  35.3 us (30%)
  matrix products  23 us (20%)
  local copies, waits for them, and re-layouts  5.55 us (5%)
  other arithmetic  2.64 us (2%)
  between operations  2.48 us (2%)
  waiting for transfers between devices  2.47 us (2%)
    psum x1, blocking collectives, local(): summed = lax.psum(local_portion * gradient, ('cond', 'gx', 'yz'))  43.9 us
    ppermute x6, starting transfers between devices, with_halo(): lax.ppermute(lax.slice_in_dim(block, block.shape[dim] - width, None, axis...  27.6 us
    dot_general x18, matrix products, apply_operator(): jnp.einsum('ec,exyz->cxyz', blocks[direction], shifted, precision=lax.Pre...  22.6 us
    ppermute x6, starting transfers between devices, with_halo(): lax.ppermute(lax.slice_in_dim(block, 0, width, axis=dim), axis, backward)  7.74 us
    unnamed x25, local copies, waits for them, and re-layouts  4.43 us
    ppermute x6, waiting for transfers between devices, with_halo(): lax.ppermute(lax.slice_in_dim(block, block.shape[dim] - width, None, axis...  2.45 us
  transfers between devices with their start and end apart: 12, of which 3 were waited for; matrix products, arithmetic and copies ran while one was open for 5% of the time, Pallas kernels for 0%

commit v1 on v0

v1 whole, which is shorter than its diff:
```python
import functools

import jax
import jax.numpy as jnp
from jax import lax
from jax.experimental import pallas as pl
from jax.experimental.pallas import tpu as pltpu
from jax.sharding import PartitionSpec as P

NDES = 4096
RELAX = 0.8
LANES = 128
PAD = 8
MESH = pl.DeviceIdType.MESH


def kernel(
    sizes,
    adjoint,
    source_hbm,
    diagonal_hbm,
    flux,
    sensitivity_hbm,
    mask_hbm,
    slots_hbm,
    basis_hbm,
    weights,
    smoothed_out,
    residual_out,
    gradient_out,
    fields,
    source,
    diagonal,
    sensitivity,
    mask,
    slots,
    basis,
    surface,
    pieces,
    arrived,
    local_sems,
    send_sems,
    recv_sems,
    piece_sems,
):
    n_cond, n_gx, n_yz = sizes
    devices = n_cond * n_gx * n_yz
    nvar, nx, ny, nz = source.shape
    halves = nz // LANES
    rows = pieces.shape[1]
    per_owner = NDES // (n_gx * n_yz)
    ci, xi, yi = lax.axis_index("cond"), lax.axis_index("gx"), lax.axis_index("yz")
    me = (ci * n_gx + xi) * n_yz + yi

    def place(flat):
        return (flat // (n_gx * n_yz), (flat // n_yz) % n_gx, flat % n_yz)

    barrier = pltpu.get_barrier_semaphore()

    def greet(step, carry):
        pl.semaphore_signal(
            barrier, inc=1, device_id=place((me + step) % devices), device_id_type=MESH
        )
        return carry

    lax.fori_loop(1, devices, greet, 0)

    loads = []

    def load(src, dst):
        copy = pltpu.make_async_copy(src, dst, local_sems.at[len(loads)])
        copy.start()
        loads.append(copy)

    for h in range(halves):
        load(
            adjoint.at[0, :, :, :, pl.ds(h * LANES, LANES)],
            fields.at[0, :, pl.ds(1, nx), h, pl.ds(PAD, ny), :],
        )
    load(source_hbm.at[0], source)
    load(diagonal_hbm, diagonal)
    first_loads = len(loads)
    load(sensitivity_hbm.at[0], sensitivity)
    load(mask_hbm, mask)
    load(slots_hbm, slots)
    load(basis_hbm, basis)

    @pl.when(xi == 0)
    def _():
        fields[:, :, 0] = jnp.zeros_like(fields[:, :, 0])

    @pl.when(xi == n_gx - 1)
    def _():
        fields[:, :, nx + 1] = jnp.zeros_like(fields[:, :, nx + 1])

    blank = jnp.zeros((3, nvar, nx, halves, 1, LANES), jnp.float32)

    @pl.when(yi == 0)
    def _():
        fields[:, :, 1 : nx + 1, :, PAD - 1 : PAD, :] = blank

    @pl.when(yi == n_yz - 1)
    def _():
        fields[:, :, 1 : nx + 1, :, PAD + ny : PAD + ny + 1, :] = blank

    def faces(stage):
        whole_x = pl.ds(1, nx)
        plans = []
        for h in range(halves):
            lanes = pl.ds(h * LANES, LANES)

            def at(x, y, stage=stage, h=h):
                return fields.at[stage, :, x, h, y, :]

            def sent(x, y, stage=stage, lanes=lanes, h=h):
                if stage == 0:
                    x0 = x - 1 if isinstance(x, int) else pl.ds(0, nx)
                    return adjoint.at[0, :, x0, pl.ds(y.start - PAD, y.size), lanes]
                return fields.at[stage, :, x, h, y, :]

            inner_y = pl.ds(PAD, ny)
            plans.append((xi < n_gx - 1, xi > 0, (ci, xi + 1, yi), sent(nx, inner_y), at(0, inner_y)))
            plans.append((xi > 0, xi < n_gx - 1, (ci, xi - 1, yi), sent(1, inner_y), at(nx + 1, inner_y)))
            plans.append((yi < n_yz - 1, yi > 0, (ci, xi, yi + 1), sent(whole_x, pl.ds(PAD + ny - 1, 1)), at(whole_x, pl.ds(PAD - 1, 1))))
            plans.append((yi > 0, yi < n_yz - 1, (ci, xi, yi - 1), sent(whole_x, pl.ds(PAD, 1)), at(whole_x, pl.ds(PAD + ny, 1))))
        out = []
        for i, (go, come, target, src, dst) in enumerate(plans):
            copy = pltpu.make_async_remote_copy(
                src_ref=src,
                dst_ref=dst,
                send_sem=send_sems.at[stage, i],
                recv_sem=recv_sems.at[stage, i],
                device_id=target,
                device_id_type=MESH,
            )
            out.append((go, come, copy))
        return out

    def begin(plans):
        for go, _, copy in plans:
            pl.when(go)(copy.start)

    def receive(plans):
        for _, come, copy in plans:
            pl.when(come)(copy.wait_recv)

    def drain(plans):
        for go, _, copy in plans:
            pl.when(go)(copy.wait_send)

    pl.semaphore_wait(barrier, devices - 1)
    exchange = [faces(stage) for stage in range(3)]
    begin(exchange[0])
    for copy in loads[:first_loads]:
        copy.wait()

    lane = lax.broadcasted_iota(jnp.int32, (ny, LANES), 1)
    spans = [slice(h * LANES, (h + 1) * LANES) for h in range(halves)]

    def gathered(stage, x):
        acc = [[source[k, x, :, s] for s in spans] for k in range(nvar)]
        centres = []
        for e in range(nvar):
            centre = [fields[stage, e, x + 1, h, PAD : PAD + ny, :] for h in range(halves)]
            centres.append(centre)
            up = [pltpu.roll(c, LANES - 1, 1) for c in centre] + [jnp.zeros((ny, LANES), jnp.float32)]
            down = [jnp.zeros((ny, LANES), jnp.float32)] + [pltpu.roll(c, 1, 1) for c in centre]
            shifted = (
                [fields[stage, e, x + 2, h, PAD : PAD + ny, :] for h in range(halves)],
                [fields[stage, e, x, h, PAD : PAD + ny, :] for h in range(halves)],
                [fields[stage, e, x + 1, h, PAD + 1 : PAD + ny + 1, :] for h in range(halves)],
                [fields[stage, e, x + 1, h, PAD - 1 : PAD + ny - 1, :] for h in range(halves)],
                [jnp.where(lane == LANES - 1, up[h + 1], up[h]) for h in range(halves)],
                [jnp.where(lane == 0, down[h], down[h + 1]) for h in range(halves)],
            )
            for d in range(6):
                for k in range(nvar):
                    scale = flux[0, d, e, k]
                    for h in range(halves):
                        acc[k][h] = acc[k][h] + scale * shifted[d][h]
        return acc, centres

    def relax(stage, x, carry):
        acc, centres = gathered(stage, x)
        step = [RELAX / diagonal[x, :, s] for s in spans]
        total = [None] * halves
        for k in range(nvar):
            for h in range(halves):
                value = (1.0 - RELAX) * centres[k][h] + step[h] * acc[k][h]
                fields[stage + 1, k, x + 1, h, PAD : PAD + ny, :] = value
                if stage == 1:
                    smoothed_out[0, k, x, :, spans[h]] = value
                    term = value * sensitivity[k, x, :, spans[h]].astype(jnp.float32)
                    total[h] = term if k == 0 else total[h] + term
        if stage == 1:
            for h in range(halves):
                surface[x, :, spans[h]] = total[h] * mask[x, :, spans[h]].astype(jnp.float32)
        return carry

    def settle(x, carry):
        acc, centres = gathered(2, x)
        for k in range(nvar):
            for h in range(halves):
                value = acc[k][h] - diagonal[x, :, spans[h]] * centres[k][h]
                residual_out[0, k, x, :, spans[h]] = value
        return carry

    receive(exchange[0])
    lax.fori_loop(0, nx, functools.partial(relax, 0), 0)
    begin(exchange[1])
    for copy in loads[first_loads:]:
        copy.wait()
    receive(exchange[1])
    lax.fori_loop(0, nx, functools.partial(relax, 1), 0)
    begin(exchange[2])

    def split(value):
        high = value.astype(jnp.bfloat16)
        return high, (value - high.astype(jnp.float32)).astype(jnp.bfloat16)

    dot = functools.partial(jnp.dot, preferred_element_type=jnp.float32)
    basis_high, basis_low = split(basis[...])
    surface_high, surface_low = split(surface[...].reshape(nx * ny, nz))
    projected = (
        dot(surface_high, basis_high) + dot(surface_high, basis_low) + dot(surface_low, basis_high)
    )
    lines = NDES // LANES
    line = lax.broadcasted_iota(jnp.int32, (lines, ny), 0)
    wanted = jnp.concatenate([2 * line, 2 * line + 1, 2 * line - 1], axis=0)
    looked = jnp.zeros((3 * lines, LANES), jnp.float32)
    for x in range(nx):
        onehot = (wanted == slots[x : x + 1, :]).astype(jnp.float32).astype(jnp.bfloat16)
        high, low = split(projected[x * ny : (x + 1) * ny])
        looked = looked + dot(onehot, high) + dot(onehot, low)
    turned = pltpu.roll(looked[lines:], LANES // 2, 1)
    column = lax.broadcasted_iota(jnp.int32, (lines, LANES), 1)
    gradient = looked[:lines] + jnp.where(column < LANES // 2, turned[lines:], turned[:lines])
    weight_sum = weights[0]
    for c in range(1, n_cond):
        weight_sum = weight_sum + weights[c]
    share = jnp.full((1, LANES), weights[ci], jnp.int32).astype(jnp.float32) / jnp.full(
        (1, LANES), weight_sum, jnp.int32
    ).astype(jnp.float32)
    gradient = gradient * share
    for g in range(lines // rows):
        pieces[g] = gradient[g * rows : (g + 1) * rows]

    def group(gx, yz):
        return (gx * n_yz + yz) * per_owner // (rows * LANES)

    def give(step, carry):
        c, gx, yz = place((me + step) % devices)
        pltpu.make_async_remote_copy(
            src_ref=pieces.at[group(gx, yz)],
            dst_ref=arrived.at[me],
            send_sem=piece_sems.at[0],
            recv_sem=piece_sems.at[1],
            device_id=(c, gx, yz),
            device_id_type=MESH,
        ).start()
        return carry

    arrived[me] = pieces[group(xi, yi)]
    lax.fori_loop(1, devices, give, 0)

    receive(exchange[2])
    lax.fori_loop(0, nx, settle, 0)

    others = arrived.at[pl.ds(0, devices - 1)]
    for i in range(2):
        pltpu.make_async_copy(others, others, piece_sems.at[i]).wait()
    gradient_out[...] = jnp.sum(arrived[...], axis=0)
    for plans in exchange:
        drain(plans)


def local(
    adjoint,
    objective_gradient,
    diagonal,
    flux_blocks,
    flux_sensitivity,
    surface_mask,
    patch_band_slot,
    design_basis,
    condition_weights,
):
    sizes = tuple(lax.axis_size(axis) for axis in ("cond", "gx", "yz"))
    devices = sizes[0] * sizes[1] * sizes[2]
    _, nvar, nx, ny, nz = adjoint.shape
    halves = nz // LANES
    per_owner = NDES // (sizes[1] * sizes[2])
    rows = max(1, per_owner // LANES)
    f32 = jnp.float32
    hbm = pl.BlockSpec(memory_space=pltpu.MemorySpace.HBM)
    smem = pl.BlockSpec(memory_space=pltpu.MemorySpace.SMEM)
    vmem = pl.BlockSpec(memory_space=pltpu.MemorySpace.VMEM)
    faces = 4 * halves
    smoothed, residual, gradient = pl.pallas_call(
        functools.partial(kernel, sizes),
        out_shape=(
            jax.ShapeDtypeStruct(adjoint.shape, f32),
            jax.ShapeDtypeStruct(adjoint.shape, f32),
            jax.ShapeDtypeStruct((rows, LANES), f32),
        ),
        in_specs=[hbm, hbm, hbm, smem, hbm, hbm, hbm, hbm, smem],
        out_specs=(vmem, vmem, vmem),
        scratch_shapes=[
            pltpu.VMEM((3, nvar, nx + 2, halves, ny + 2 * PAD, LANES), f32),
            pltpu.VMEM((nvar, nx, ny, nz), f32),
            pltpu.VMEM((nx, ny, nz), f32),
            pltpu.VMEM((nvar, nx, ny, nz), jnp.bfloat16),
            pltpu.VMEM((nx, ny, nz), jnp.int32),
            pltpu.VMEM((nx, ny), jnp.int32),
            pltpu.VMEM(design_basis.shape, f32),
            pltpu.VMEM((nx, ny, nz), f32),
            pltpu.VMEM((NDES // (rows * LANES), rows, LANES), f32),
            pltpu.VMEM((devices, rows, LANES), f32),
            pltpu.SemaphoreType.DMA((6 + halves,)),
            pltpu.SemaphoreType.DMA((3, faces)),
            pltpu.SemaphoreType.DMA((3, faces)),
            pltpu.SemaphoreType.DMA((2,)),
        ],
        compiler_params=pltpu.CompilerParams(
            collective_id=0, has_side_effects=True
        ),
    )(
        adjoint,
        objective_gradient,
        diagonal,
        flux_blocks,
        flux_sensitivity,
        surface_mask,
        patch_band_slot,
        design_basis,
        condition_weights,
    )
    flat = gradient.reshape(-1)
    if per_owner < flat.shape[0]:
        owner = lax.axis_index(("gx", "yz"))
        flat = lax.dynamic_slice_in_dim(flat, (owner * per_owner) % flat.shape[0], per_owner, 0)
    return smoothed, residual, flat


def solution(mesh):
    placed = (
        P("cond", None, "gx", "yz", None),
        P("cond", None, "gx", "yz", None),
        P("gx", "yz", None),
        P("cond", None, None, None),
        P("cond", None, "gx", "yz", None),
        P("gx", "yz", None),
        P("gx", "yz"),
        P(),
        P(),
    )
    return jax.shard_map(
        local,
        mesh=mesh,
        in_specs=placed,
        out_specs=(
            P("cond", None, "gx", "yz", None),
            P("cond", None, "gx", "yz", None),
            P(("gx", "yz")),
        ),
        check_vma=False,
    )
```

time: 116 us -> 30.5 us (0.26)
  blocking collectives: 43.9 us -> 0 us
  starting transfers between devices: 35.3 us -> 0 us
  Pallas kernels: 0 us -> 24.6 us
  matrix products: 23 us -> 0 us
  other arithmetic: 2.64 us -> 0 us
  waiting for transfers between devices: 2.47 us -> 0 us
  between operations: 2.48 us -> 0.65 us
    psum x1 -> x0, blocking collectives: 43.9 us -> none  [local(): summed = lax.psum(local_portion * gradient, ('cond', 'gx', 'yz'))]
    ppermute x12 -> x0, starting transfers between devices: 35.3 us -> none  [the longest x6 27.6 us: with_halo(): lax.ppermute(lax.slice_in_dim(block, block.shape[dim] - width, None, axis...]
    pallas_call x0 -> x1, Pallas kernels: none -> 24.6 us  [local(): pl.pallas_call(functools.partial(kernel, sizes), out_shape=(jax.ShapeDtyp...]
    dot_general x20 -> x0, matrix products: 23 us -> none  [the longest x18 22.6 us: apply_operator(): jnp.einsum('ec,exyz->cxyz', blocks[direction], shifted, precision=lax.Pre...]
    ppermute x12 -> x0, waiting for transfers between devices: 2.47 us -> none  [the longest x6 2.45 us: with_halo(): lax.ppermute(lax.slice_in_dim(block, block.shape[dim] - width, None, axis...]
    concatenate x6 -> x0, other arithmetic: 1.99 us -> none  [with_halo(): block = jnp.concatenate([low, block, high], axis=dim)]
    unnamed x25 -> x8, local copies, waits for them, and re-layouts: 4.43 us -> 4.9 us
  transfers between devices with their start and end apart: 12 -> 0, of which waited for: 3 -> 0; matrix products, arithmetic and copies ran while one was open for 5% -> 0% of each run, Pallas kernels for 0% -> 0%
where the time goes in v1:
time: 30.5 us; the launch traced here: 30.1 us
  Pallas kernels  24.6 us (81%)
  local copies, waits for them, and re-layouts  4.9 us (16%)
  between operations  0.65 us (2%)
    pallas_call x1, Pallas kernels, local(): pl.pallas_call(functools.partial(kernel, sizes), out_shape=(jax.ShapeDtyp...  24.6 us
    unnamed x8, local copies, waits for them, and re-layouts  4.9 us

profile of v1, /device:TPU:0, one launch (start us, length us, event | category | flops | bytes accessed | tf_op | source)
XLA Modules:
  0.0 30.1 jit_solution(245463272698790310)
XLA Ops:
  0.6 1.4 %copy.12.flux = f32[1,6,5,5]{3,2,1,0:T(8,128)} copy(f32[1,6,5,5]{1,0,3,2:T(1,128)} %param.12) | data formatting | bytes 1200 | tf_op args[3]
  2.1 24.6 %shard_map.112 = (f32[1,5,8,16,256]{4,3,2,1,0:T(8,128)}, f32[1,5,8,16,256]{4,3,2,1,0:T(8,128)}, f32[2,128]{1,0:T(2,128)}) custom-call(f32[1,5,8,16,256]{4,3,2,1,0:T(8,128)} %adjoint.1, f32[1,5,8,16,256]{4,3,2,1,0:T(8,128)} %source_hbm.1, f32[8,16,256]{2,1,0:T(8,128)} %diagonal_hbm.1, f32[1,6,5,5]{3,2,1,0:T(8,128)} %copy.12.flux, ...), custom_call_target="tpu_custom_call" | custom-call | tf_op jit(solution)/shard_map/pallas_call | solution.py:299
  26.7 0.0 copy-start
  26.7 2.1 %copy.16 = f32[1,5,8,16,256]{4,3,2,1,0:T(8,128)} copy(f32[1,5,8,16,256]{4,3,2,1,0:T(8,128)} %get-tuple-element.12) | data formatting | bytes 1310720
  28.7 0.0 copy-done
  28.7 0.0 copy-start.1
  28.7 0.8 %copy.17 = f32[1,5,8,16,256]{4,3,2,1,0:T(8,128)} copy(f32[1,5,8,16,256]{4,3,2,1,0:T(8,128)S(1)} %copy-done) | data formatting | bytes 1310720
  29.6 0.0 copy-done.1
  29.6 0.6 %copy.18 = f32[256]{0:T(256)} copy(f32[256]{0:T(256)S(1)} %bitcast.1) | data formatting | bytes 2048
Async XLA Ops:
  26.7 2.1 %copy-start = (f32[1,5,8,16,256]{4,3,2,1,0:T(8,128)S(1)}, f32[1,5,8,16,256]{4,3,2,1,0:T(8,128)}, u32[]{:S(2)}) copy-start(f32[1,5,8,16,256]{4,3,2,1,0:T(8,128)} %get-tuple-element.13) | copy-start | bytes 1966084
  28.7 0.8 %copy-start.1 = (f32[2,128]{1,0:T(2,128)S(1)}, f32[2,128]{1,0:T(2,128)}, u32[]{:S(2)}) copy-start(f32[2,128]{1,0:T(2,128)} %get-tuple-element.8) | copy-start | bytes 3076

commit v2 on v1

--- a/solution.py
+++ b/solution.py
@@ -39,8 +39,10 @@
     pieces,
     arrived,
     local_sems,
-    send_sems,
-    recv_sems,
+    plane_sems,
+    first_sems,
+    row_sems,
+    face_sems,
     piece_sems,
 ):
     n_cond, n_gx, n_yz = sizes
@@ -57,84 +59,136 @@
 
     barrier = pltpu.get_barrier_semaphore()
 
-    def greet(step, carry):
-        pl.semaphore_signal(
-            barrier, inc=1, device_id=place((me + step) % devices), device_id_type=MESH
+    def for_others(action):
+        if devices <= 64:
+            here = (ci, xi, yi)
+            turns = [[(p + t) % n for t in range(n)] for p, n in zip(here, sizes)]
+            for dy in range(n_yz):
+                for dx in range(n_gx):
+                    for dc in range(n_cond):
+                        if dc or dx or dy:
+                            action(turns[0][dc], turns[1][dx], turns[2][dy])
+        else:
+
+            def step(t, carry):
+                action(*place((me + t) % devices))
+                return carry
+
+            lax.fori_loop(1, devices, step, 0)
+
+    def greet(c, gx, yz):
+        pl.semaphore_signal(barrier, inc=1, device_id=(c, gx, yz), device_id_type=MESH)
+
+    for_others(greet)
+    inner_y = pl.ds(PAD, ny)
+
+    def plane_loads(x):
+        pairs = [
+            (
+                adjoint.at[0, :, x, :, pl.ds(h * LANES, LANES)],
+                fields.at[0, :, x + 1, h, inner_y, :],
+            )
+            for h in range(halves)
+        ]
+        pairs.append((source_hbm.at[0, :, x], source.at[:, x]))
+        pairs.append((diagonal_hbm.at[x], diagonal.at[x]))
+        return [
+            pltpu.make_async_copy(src, dst, plane_sems.at[i, x])
+            for i, (src, dst) in enumerate(pairs)
+        ]
+
+    late_loads = [
+        pltpu.make_async_copy(src, dst, local_sems.at[i])
+        for i, (src, dst) in enumerate(
+            (
+                (sensitivity_hbm.at[0], sensitivity),
+                (mask_hbm, mask),
+                (slots_hbm, slots),
+                (basis_hbm, basis),
+            )
         )
-        return carry
-
-    lax.fori_loop(1, devices, greet, 0)
-
-    loads = []
-
-    def load(src, dst):
-        copy = pltpu.make_async_copy(src, dst, local_sems.at[len(loads)])
+    ]
+    for x in range(nx):
+        for copy in plane_loads(x):
+            copy.start()
+    for copy in late_loads:
         copy.start()
-        loads.append(copy)
-
+
+    has_before_x, has_after_x = xi > 0, xi < n_gx - 1
+    has_before_y, has_after_y = yi > 0, yi < n_yz - 1
+
+    blank_x = jnp.zeros((nvar, halves, ny, LANES), jnp.float32)
+    blank_y = jnp.zeros((nvar, nx, halves, 1, LANES), jnp.float32)
+
+    def clear_x(stage, x):
+        fields[stage, :, x, :, PAD : PAD + ny, :] = blank_x
+
+    def clear_y(stage, y):
+        fields[stage, :, 1 : nx + 1, :, y : y + 1, :] = blank_y
+
+    for stage in range(3):
+        pl.when(xi == 0)(functools.partial(clear_x, stage, 0))
+        pl.when(xi == n_gx - 1)(functools.partial(clear_x, stage, nx + 1))
+        pl.when(yi == 0)(functools.partial(clear_y, stage, PAD - 1))
+        pl.when(yi == n_yz - 1)(functools.partial(clear_y, stage, PAD + ny))
+
+    def remote(src, dst, sems, target):
+        return pltpu.make_async_remote_copy(
+            src_ref=src,
+            dst_ref=dst,
+            send_sem=sems[0],
+            recv_sem=sems[1],
+            device_id=target,
+            device_id_type=MESH,
+        )
+
+    after_x, before_x = (ci, xi + 1, yi), (ci, xi - 1, yi)
+    after_y, before_y = (ci, xi, yi + 1), (ci, xi, yi - 1)
+
+    first_y, first_x = [], []
     for h in range(halves):
-        load(
-            adjoint.at[0, :, :, :, pl.ds(h * LANES, LANES)],
-            fields.at[0, :, pl.ds(1, nx), h, pl.ds(PAD, ny), :],
-        )
-    load(source_hbm.at[0], source)
-    load(diagonal_hbm, diagonal)
-    first_loads = len(loads)
-    load(sensitivity_hbm.at[0], sensitivity)
-    load(mask_hbm, mask)
-    load(slots_hbm, slots)
-    load(basis_hbm, basis)
-
-    @pl.when(xi == 0)
-    def _():
-        fields[:, :, 0] = jnp.zeros_like(fields[:, :, 0])
-
-    @pl.when(xi == n_gx - 1)
-    def _():
-        fields[:, :, nx + 1] = jnp.zeros_like(fields[:, :, nx + 1])
-
-    blank = jnp.zeros((3, nvar, nx, halves, 1, LANES), jnp.float32)
-
-    @pl.when(yi == 0)
-    def _():
-        fields[:, :, 1 : nx + 1, :, PAD - 1 : PAD, :] = blank
-
-    @pl.when(yi == n_yz - 1)
-    def _():
-        fields[:, :, 1 : nx + 1, :, PAD + ny : PAD + ny + 1, :] = blank
-
-    def faces(stage):
-        whole_x = pl.ds(1, nx)
-        plans = []
-        for h in range(halves):
-            lanes = pl.ds(h * LANES, LANES)
-
-            def at(x, y, stage=stage, h=h):
-                return fields.at[stage, :, x, h, y, :]
-
-            def sent(x, y, stage=stage, lanes=lanes, h=h):
-                if stage == 0:
-                    x0 = x - 1 if isinstance(x, int) else pl.ds(0, nx)
-                    return adjoint.at[0, :, x0, pl.ds(y.start - PAD, y.size), lanes]
-                return fields.at[stage, :, x, h, y, :]
-
-            inner_y = pl.ds(PAD, ny)
-            plans.append((xi < n_gx - 1, xi > 0, (ci, xi + 1, yi), sent(nx, inner_y), at(0, inner_y)))
-            plans.append((xi > 0, xi < n_gx - 1, (ci, xi - 1, yi), sent(1, inner_y), at(nx + 1, inner_y)))
-            plans.append((yi < n_yz - 1, yi > 0, (ci, xi, yi + 1), sent(whole_x, pl.ds(PAD + ny - 1, 1)), at(whole_x, pl.ds(PAD - 1, 1))))
-            plans.append((yi > 0, yi < n_yz - 1, (ci, xi, yi - 1), sent(whole_x, pl.ds(PAD, 1)), at(whole_x, pl.ds(PAD + ny, 1))))
-        out = []
-        for i, (go, come, target, src, dst) in enumerate(plans):
-            copy = pltpu.make_async_remote_copy(
-                src_ref=src,
-                dst_ref=dst,
-                send_sem=send_sems.at[stage, i],
-                recv_sem=recv_sems.at[stage, i],
-                device_id=target,
-                device_id_type=MESH,
-            )
-            out.append((go, come, copy))
-        return out
+        lanes = pl.ds(h * LANES, LANES)
+
+        def sems(way, h=h):
+            return first_sems.at[0, way, h], first_sems.at[1, way, h]
+
+        inner_x = pl.ds(1, nx)
+        first_y.append((has_after_y, has_before_y, remote(
+            adjoint.at[0, :, :, pl.ds(ny - 1, 1), lanes],
+            fields.at[0, :, inner_x, h, pl.ds(PAD - 1, 1), :], sems(0), after_y)))
+        first_y.append((has_before_y, has_after_y, remote(
+            adjoint.at[0, :, :, pl.ds(0, 1), lanes],
+            fields.at[0, :, inner_x, h, pl.ds(PAD + ny, 1), :], sems(1), before_y)))
+        first_x.append((has_after_x, has_before_x, remote(
+            adjoint.at[0, :, nx - 1, :, lanes],
+            fields.at[0, :, 0, h, inner_y, :], sems(2), after_x)))
+        first_x.append((has_before_x, has_after_x, remote(
+            adjoint.at[0, :, 0, :, lanes],
+            fields.at[0, :, nx + 1, h, inner_y, :], sems(3), before_x)))
+
+    def row_copies(stage, x):
+        def sems(way):
+            return row_sems.at[stage - 1, 0, way, x], row_sems.at[stage - 1, 1, way, x]
+
+        def row(y):
+            return fields.at[stage, :, x + 1, :, pl.ds(y, 1), :]
+
+        return [
+            (has_after_y, has_before_y, remote(row(PAD + ny - 1), row(PAD - 1), sems(0), after_y)),
+            (has_before_y, has_after_y, remote(row(PAD), row(PAD + ny), sems(1), before_y)),
+        ]
+
+    def face_copies(stage):
+        def sems(way):
+            return face_sems.at[stage - 1, 0, way], face_sems.at[stage - 1, 1, way]
+
+        def face(x):
+            return fields.at[stage, :, x, :, inner_y, :]
+
+        return [
+            (has_after_x, has_before_x, remote(face(nx), face(0), sems(0), after_x)),
+            (has_before_x, has_after_x, remote(face(1), face(nx + 1), sems(1), before_x)),
+        ]
 
     def begin(plans):
         for go, _, copy in plans:
@@ -149,10 +203,11 @@
             pl.when(go)(copy.wait_send)
 
     pl.semaphore_wait(barrier, devices - 1)
-    exchange = [faces(stage) for stage in range(3)]
-    begin(exchange[0])
-    for copy in loads[:first_loads]:
-        copy.wait()
+    begin(first_y)
+    begin(first_x)
+
+    def plane_of(step):
+        return jnp.where(step < nx - 2, step + 1, jnp.where(step == nx - 2, 0, nx - 1))
 
     lane = lax.broadcasted_iota(jnp.int32, (ny, LANES), 1)
     spans = [slice(h * LANES, (h + 1) * LANES) for h in range(halves)]
@@ -175,12 +230,31 @@
             )
             for d in range(6):
                 for k in range(nvar):
-                    scale = flux[0, d, e, k]
+                    scale = flux[e, k, 0, d]
                     for h in range(halves):
                         acc[k][h] = acc[k][h] + scale * shifted[d][h]
         return acc, centres
 
-    def relax(stage, x, carry):
+    def ready(stage, step):
+        x = plane_of(step)
+        if stage == 0:
+
+            @pl.when(step < nx - 2)
+            def _():
+                for copy in plane_loads(step + 2):
+                    copy.wait()
+
+        else:
+            receive(row_copies(stage, x))
+
+        @pl.when(step == nx - 2)
+        def _():
+            receive(first_x if stage == 0 else face_copies(stage))
+
+        return x
+
+    def relax(stage, step_index, carry):
+        x = ready(stage, step_index)
         acc, centres = gathered(stage, x)
         step = [RELAX / diagonal[x, :, s] for s in spans]
         total = [None] * halves
@@ -195,9 +269,14 @@
         if stage == 1:
             for h in range(halves):
                 surface[x, :, spans[h]] = total[h] * mask[x, :, spans[h]].astype(jnp.float32)
+        begin(row_copies(stage + 1, x))
+        up_face, down_face = face_copies(stage + 1)
+        pl.when(x == nx - 1)(functools.partial(begin, [up_face]))
+        pl.when(x == 0)(functools.partial(begin, [down_face]))
         return carry
 
-    def settle(x, carry):
+    def settle(step_index, carry):
+        x = ready(2, step_index)
         acc, centres = gathered(2, x)
         for k in range(nvar):
             for h in range(halves):
@@ -205,14 +284,14 @@
                 residual_out[0, k, x, :, spans[h]] = value
         return carry
 
-    receive(exchange[0])
+    for x in range(2):
+        for copy in plane_loads(x):
+            copy.wait()
+    receive(first_y)
     lax.fori_loop(0, nx, functools.partial(relax, 0), 0)
-    begin(exchange[1])
-    for copy in loads[first_loads:]:
+    for copy in late_loads:
         copy.wait()
-    receive(exchange[1])
     lax.fori_loop(0, nx, functools.partial(relax, 1), 0)
-    begin(exchange[2])
 
     def split(value):
         high = value.astype(jnp.bfloat16)
@@ -248,30 +327,32 @@
     def group(gx, yz):
         return (gx * n_yz + yz) * per_owner // (rows * LANES)
 
-    def give(step, carry):
-        c, gx, yz = place((me + step) % devices)
-        pltpu.make_async_remote_copy(
-            src_ref=pieces.at[group(gx, yz)],
-            dst_ref=arrived.at[me],
-            send_sem=piece_sems.at[0],
-            recv_sem=piece_sems.at[1],
-            device_id=(c, gx, yz),
-            device_id_type=MESH,
+    def give(c, gx, yz):
+        remote(
+            pieces.at[group(gx, yz)],
+            arrived.at[me],
+            (piece_sems.at[0], piece_sems.at[1]),
+            (c, gx, yz),
         ).start()
-        return carry
 
     arrived[me] = pieces[group(xi, yi)]
-    lax.fori_loop(1, devices, give, 0)
-
-    receive(exchange[2])
+    for_others(give)
     lax.fori_loop(0, nx, settle, 0)
 
     others = arrived.at[pl.ds(0, devices - 1)]
     for i in range(2):
         pltpu.make_async_copy(others, others, piece_sems.at[i]).wait()
     gradient_out[...] = jnp.sum(arrived[...], axis=0)
-    for plans in exchange:
-        drain(plans)
+    drain(first_y)
+    drain(first_x)
+    for stage in (1, 2):
+        drain(face_copies(stage))
+
+        def drain_row(x, carry, stage=stage):
+            drain(row_copies(stage, x))
+            return carry
+
+        lax.fori_loop(0, nx, drain_row, 0)
 
 
 def local(
@@ -295,13 +376,12 @@
     hbm = pl.BlockSpec(memory_space=pltpu.MemorySpace.HBM)
     smem = pl.BlockSpec(memory_space=pltpu.MemorySpace.SMEM)
     vmem = pl.BlockSpec(memory_space=pltpu.MemorySpace.VMEM)
-    faces = 4 * halves
     smoothed, residual, gradient = pl.pallas_call(
         functools.partial(kernel, sizes),
         out_shape=(
-            jax.ShapeDtypeStruct(adjoint.shape, f32),
-            jax.ShapeDtypeStruct(adjoint.shape, f32),
-            jax.ShapeDtypeStruct((rows, LANES), f32),
+            pltpu.VMEM(adjoint.shape, f32),
+            pltpu.VMEM(adjoint.shape, f32),
+            pltpu.VMEM((rows, LANES), f32),
         ),
         in_specs=[hbm, hbm, hbm, smem, hbm, hbm, hbm, hbm, smem],
         out_specs=(vmem, vmem, vmem),
@@ -316,19 +396,21 @@
             pltpu.VMEM((nx, ny, nz), f32),
             pltpu.VMEM((NDES // (rows * LANES), rows, LANES), f32),
             pltpu.VMEM((devices, rows, LANES), f32),
-            pltpu.SemaphoreType.DMA((6 + halves,)),
-            pltpu.SemaphoreType.DMA((3, faces)),
-            pltpu.SemaphoreType.DMA((3, faces)),
+            pltpu.SemaphoreType.DMA((4,)),
+            pltpu.SemaphoreType.DMA((2 + halves, nx)),
+            pltpu.SemaphoreType.DMA((2, 4, halves)),
+            pltpu.SemaphoreType.DMA((2, 2, 2, nx)),
+            pltpu.SemaphoreType.DMA((2, 2, 2)),
             pltpu.SemaphoreType.DMA((2,)),
         ],
         compiler_params=pltpu.CompilerParams(
-            collective_id=0, has_side_effects=True
+            collective_id=0, has_side_effects=True, vmem_limit_bytes=67043328 - 2 * adjoint.size * 4 - 2**16
         ),
     )(
         adjoint,
         objective_gradient,
         diagonal,
-        flux_blocks,
+        jnp.transpose(flux_blocks, (2, 3, 0, 1)),
         flux_sensitivity,
         surface_mask,
         patch_band_slot,

time: 30.5 us -> 24.5 us (0.80)
  Pallas kernels: 24.6 us -> 21.4 us
  local copies, waits for them, and re-layouts: 4.9 us -> 2.24 us
    pallas_call x1, Pallas kernels: 24.6 us -> 21.4 us  [local(): pl.pallas_call(functools.partial(kernel, sizes), out_shape=(pltpu.VMEM(ad...]
    unnamed x8 -> x3, local copies, waits for them, and re-layouts: 4.9 us -> 2.24 us
where the time goes in v2:
time: 24.5 us; the launch traced here: 24.3 us
  Pallas kernels  21.4 us (87%)
  local copies, waits for them, and re-layouts  2.24 us (9%)
  between operations  0.64 us (3%)
    pallas_call x1, Pallas kernels, local(): pl.pallas_call(functools.partial(kernel, sizes), out_shape=(pltpu.VMEM(ad...  21.4 us
    unnamed x3, local copies, waits for them, and re-layouts  2.24 us

profile of v2, /device:TPU:0, one launch (start us, length us, event | category | flops | bytes accessed | tf_op | source)
XLA Modules:
  0.0 24.3 jit_solution(15123942980295389175)
XLA Ops:
  0.6 21.4 %shard_map.112 = (f32[1,5,8,16,256]{4,3,2,1,0:T(8,128)S(1)}, f32[1,5,8,16,256]{4,3,2,1,0:T(8,128)S(1)}, f32[2,128]{1,0:T(2,128)S(1)}) custom-call(f32[1,5,8,16,256]{4,3,2,1,0:T(8,128)} %adjoint.1, f32[1,5,8,16,256]{4,3,2,1,0:T(8,128)} %source_hbm.1, f32[8,16,256]{2,1,0:T(8,128)} %diagonal_hbm.1, f32[5,5,1,6]{3,2,1,0:T(1,128)} %bitcast.3, ...), custom_call_target="tpu_custom_call" | custom-call | tf_op jit(solution)/shard_map/pallas_call | solution.py:379
  22.0 0.8 %copy.15 = f32[1,5,8,16,256]{4,3,2,1,0:T(8,128)} copy(f32[1,5,8,16,256]{4,3,2,1,0:T(8,128)S(1)} %get-tuple-element.9) | data formatting | bytes 1310720
  22.9 0.6 %copy.17 = f32[256]{0:T(256)} copy(f32[256]{0:T(256)S(1)} %bitcast.2) | data formatting | bytes 2048
  23.4 0.8 %copy.16 = f32[1,5,8,16,256]{4,3,2,1,0:T(8,128)} copy(f32[1,5,8,16,256]{4,3,2,1,0:T(8,128)S(1)} %get-tuple-element.10) | data formatting | bytes 1310720
